TPU v7x, 128 devices: a whole 4x4x4 slice. The times are simulated.
128 devices in a mesh: batch: 32 (over z, y_hi, x), head: 4 (over y_lo, core).
Axes of the slice: x: 4, y: 4 (y_hi: 2, y_lo: 2; y = y_hi * 2 + y_lo), z: 4, core: 2. Of those that a mesh axis runs over, the one named last changes fastest.
Arguments:
- features: bfloat16 [4096, 24, 512], P(('batch', 'head')), may hold values from -6 to 6
- state_h: bfloat16 [4096, 1024], P(('batch', 'head')), may hold values from -0.8984375 to 0.8984375
- state_c: bfloat16 [4096, 1024], P(('batch', 'head')), may hold values from -4 to 4
- valid: int32 [4096], P(('batch', 'head')), may hold values 0 or 1
- ends: int32 [4096, 24], P(('batch', 'head')), may hold values 0 or 1
- policy: int32 [4096, 1], P(('batch', 'head')), may hold values from 0 to 31; in each aligned block of 32 rows (0 to 31, 32 to 63, ...) at most 2 rows name the same one
- actions: int32 [4096, 16], P(('batch', 'head')), may hold values from 0 to 17
- w_input: bfloat16 [512, 4, 1024], P('batch', None, 'head'), may hold values from -0.25 to 0.25
- w_recur: bfloat16 [1024, 4, 1024], P('batch', None, 'head'), may hold values from -0.1875 to 0.1875
- lstm_bias: float32 [4, 1024], replicated, may hold values from -3 to 5
- w_hidden: bfloat16 [32, 1024, 1024], P('head'), may hold values from -0.1875 to 0.1875
- w_value: bfloat16 [32, 512], P('head'), may hold values from -0.25 to 0.25
- w_advantage: bfloat16 [32, 512, 18], P('head'), may hold values from -0.25 to 0.25
Outputs:
- q_values: float32 [4096, 16, 18], P(('batch', 'head'))
- q_taken: float32 [4096, 16], P(('batch', 'head'))
Inputs may be any that keep to these rules, and one draw needn't show every extreme that they name: In the rows of one device no policy appears more than 2 times, and some policy appears exactly 2 times.
All inputs are finite; a program needn't handle non-finite values. No bound on the sum of `valid` or of `ends` on one device may be relied on, other than what follows from the above.
Results may differ from a plain program's by a relative error of at most 0.007.
Values may be sent and summed in bfloat16 or wider, within the bound.
A program may use at most 128 MiB of HBM per device.

v0:
```python
import jax
import jax.numpy as jnp
from jax import lax
from jax.sharding import PartitionSpec as P

ACTIONS = 18
POLICIES = 32
CAPP = 2


def in_one_piece(arrays, axis, dim, along):
    widths = [a.shape[along] for a in arrays]
    both = jnp.concatenate(arrays, axis=along)
    filled = lax.all_gather(both, axis, axis=dim, tiled=True)
    return tuple(jnp.split(filled, [sum(widths[:k]) for k in range(1, len(widths))], axis=along))


def slot_table(owners, per_source, capacity, policies):
    count = owners.shape[0]
    sources = count // per_source
    place = jnp.arange(count, dtype=jnp.int32)
    anchor = place // per_source
    before = (
        (owners[:, None] == owners[None, :])
        & (anchor[:, None] == anchor[None, :])
        & (place[None, :] < place[:, None])
    )
    rank = jnp.sum(before.astype(jnp.int32), axis=1)
    target = owners * (sources * capacity) + anchor * capacity + rank
    total = policies * sources * capacity
    return (jnp.arange(total, dtype=jnp.int32)[:, None] == target[None, :]).astype(jnp.bfloat16)


def lstm_cell(pre_t, full_h, cell_state, keep_t, w_flat, bias, width):
    full_h = full_h * keep_t[:, None].astype(jnp.bfloat16)
    cell_state = cell_state * keep_t[:, None]
    gates = (
        pre_t
        + jnp.dot(full_h, w_flat, preferred_element_type=jnp.float32).reshape(-1, 4, width)
        + bias
    )
    cell_state = jax.nn.sigmoid(gates[:, 1]) * cell_state + jax.nn.sigmoid(gates[:, 0]) * jnp.tanh(
        gates[:, 2]
    )
    new_h = (jax.nn.sigmoid(gates[:, 3]) * jnp.tanh(cell_state)).astype(jnp.bfloat16)
    return (new_h, cell_state)


def shards(
    features,
    state_h,
    state_c,
    valid,
    ends,
    policy,
    actions,
    w_input,
    w_recur,
    lstm_bias,
    w_hidden,
    w_value,
    w_advantage,
):
    seq_dev, steps, width_e = features.shape
    width_h = state_h.shape[1]
    learn = actions.shape[1]
    burn = steps - learn
    keep_start = valid.astype(jnp.bfloat16)[:, None]
    start_h = state_h * keep_start
    start_c = state_c * keep_start
    w_in_rows, w_rec_rows = in_one_piece((w_input, w_recur), "head", 2, 0)
    feat_flat = features.transpose(1, 0, 2).reshape(-1, width_e)
    w_in_full = lax.all_gather(w_in_rows, "batch", axis=0, tiled=True).reshape(width_e, 4 * width_h)
    pre = jnp.dot(feat_flat, w_in_full, preferred_element_type=jnp.float32).reshape(
        steps, seq_dev, 4, width_h
    )
    w_flat = lax.all_gather(w_rec_rows, "batch", axis=0, tiled=True).reshape(width_h, 4 * width_h)
    keeps = 1.0 - ends.astype(jnp.float32).T

    def advance(carry, inputs):
        full_h, cell_state = carry
        pre_t, keep_t = inputs
        new_h, cell_state = lstm_cell(pre_t, full_h, cell_state, keep_t, w_flat, lstm_bias, width_h)
        return ((new_h, cell_state), new_h)

    _, outputs = lax.scan(advance, (start_h, start_c.astype(jnp.float32)), (pre, keeps))
    learned = outputs[burn:]
    table = slot_table(policy[:, 0], seq_dev, CAPP, POLICIES)
    packed = jnp.einsum("ks,tsu->ktu", table, learned, preferred_element_type=jnp.float32).astype(
        jnp.bfloat16
    )
    packed = packed.reshape(POLICIES, CAPP, learn, width_h)
    routed = lax.all_to_all(packed, "head", split_axis=0, concat_axis=1, tiled=True)
    local_heads, slots = (routed.shape[0], routed.shape[1])
    rows = routed.reshape(local_heads, slots * learn, width_h)
    mid = jnp.einsum("prh,phk->prk", rows, w_hidden, preferred_element_type=jnp.float32)
    mid = jnp.maximum(mid, 0.0).astype(jnp.bfloat16)
    branch = w_value.shape[1]
    value = jnp.einsum(
        "prk,pk->pr", mid[:, :, :branch], w_value, preferred_element_type=jnp.float32
    )
    advantage = jnp.einsum(
        "prk,pka->pra", mid[:, :, branch:], w_advantage, preferred_element_type=jnp.float32
    )
    q_local = value[:, :, None] + advantage - jnp.mean(advantage, axis=-1, keepdims=True)
    q_local = q_local.reshape(local_heads, slots, learn, ACTIONS)
    returned = lax.all_to_all(
        q_local.astype(jnp.bfloat16), "head", split_axis=1, concat_axis=0, tiled=True
    ).astype(q_local.dtype)
    own_table = slot_table(policy[:, 0], seq_dev, CAPP, POLICIES).astype(jnp.float32)
    q_values = jnp.dot(
        own_table.T,
        returned.reshape(POLICIES * CAPP, learn * ACTIONS),
        precision=lax.Precision.HIGHEST,
    ).reshape(seq_dev, learn, ACTIONS)
    chosen = actions[:, :, None] == jnp.arange(ACTIONS, dtype=jnp.int32)[None, None, :]
    q_taken = jnp.sum(jnp.where(chosen, q_values, 0.0), axis=-1)
    return (q_values, q_taken)


def solution(mesh):
    return jax.shard_map(
        shards,
        mesh=mesh,
        in_specs=(
            P(("batch", "head"), None, None),
            P(("batch", "head"), None),
            P(("batch", "head"), None),
            P(("batch", "head")),
            P(("batch", "head"), None),
            P(("batch", "head"), None),
            P(("batch", "head"), None),
            P("batch", None, "head"),
            P("batch", None, "head"),
            P(),
            P("head", None, None),
            P("head", None),
            P("head", None, None),
        ),
        out_specs=(P(("batch", "head"), None, None), P(("batch", "head"), None)),
        check_vma=False,
    )
```

profile of v0, /device:TPU:1, one launch (start us, length us, event | category | flops | bytes accessed | tf_op | source)
XLA Modules:
  0.0 450.7 jit_solution(334485971511818191)
XLA Ops:
  7.3 1.0 pad_maximum_fusion
  8.3 7.9 %all_gather.9 = bf16[48,4,1024]{2,1,0:T(4,128)(2,1)S(1)} all-gather(bf16[48,4,256]{2,1,0:T(4,128)(2,1)S(1)} %pad_maximum_fusion), channel_id=1, replica_groups=mesh['batch'=32,'head'=4] {'head'}, dimensions={2}, use_global_device_ids=true | all-gather | bytes 491520 | tf_op jit(solution)/shard_map/all_gather | solution.py:14
  18.4 79.2 %all-gather.3.cloned.1.call-done = bf16[512,4,1024]{2,1,0:T(4,128)(2,1)} async-done(((bf16[16,4,1024]{2,1,0:T(4,128)(2,1)}), bf16[512,4,1024]{2,1,0:T(4,128)(2,1)}) %all-gather.3.cloned.1.call-update) | async-done | bytes 4194320 | tf_op jit(solution)/shard_map/all_gather | solution.py:73
  97.6 4.5 copy.61
  102.1 6.6 %convolution_bitcast_fusion = f32[768,4096]{0,1:T(8,128)} fusion(bf16[512,4096]{1,0:T(8,128)(2,1)S(1)} %bitcast.92, bf16[768,512]{1,0:T(8,128)(2,1)S(1)} %bitcast.96), kind=kOutput, calls=%fused_computation.30 | convolution fusion | flops 3221225472 | bytes 17563648 | tf_op jit(solution)/shard_map/dot_general | solution.py:74
  108.7 12.7 %copy.47 = f32[768,4096]{1,0:T(8,128)} copy(f32[768,4096]{0,1:T(8,128)} %convolution_bitcast_fusion) | data formatting | bytes 25165824 | tf_op jit(solution)/shard_map/dot_general | solution.py:74
  121.3 15.6 %reshape.110 = f32[24,32,4,1024]{3,2,1,0:T(4,128)} reshape(f32[768,4096]{1,0:T(8,128)} %copy.47) | data formatting | bytes 25165824 | tf_op jit(solution)/shard_map/reshape | solution.py:74
  137.0 65.1 %all-gather.5.cloned.1.call-done = bf16[1024,4,1024]{2,1,0:T(4,128)(2,1)} async-done(((bf16[32,4,1024]{2,1,0:T(4,128)(2,1)}), bf16[1024,4,1024]{2,1,0:T(4,128)(2,1)}) %all-gather.5.cloned.1.call-update) | async-done | bytes 8388624 | tf_op jit(solution)/shard_map/all_gather | solution.py:77
  202.1 12.1 %copy.62 = bf16[128,8,4,1024]{3,1,2,0:T(8,128)(2,1)} copy(bf16[128,8,4,1024]{3,2,1,0:T(4,128)(2,1)} %bitcast.89) | data formatting | bytes 16777216
  214.2 173.0 %while.14 = (s32[]{:T(128)}, bf16[32,1024]{1,0:T(8,128)(2,1)S(1)}, f32[32,1024]{1,0:T(8,128)S(1)}, bf16[24,32,1024]{2,1,0:T(8,128)(2,1)}, f32[24,32,4,1024]{3,2,...) while((s32[]{:T(128)}, bf16[32,1024]{1,0:T(8,128)(2,1)S(1)}, ...), condition=%wide.region_2.3_spmd, body=%wide.region_1.2_spmd.sunk | while | flops 269221920 | bytes 12534885 | solution.py:86
  214.2 5.0 %fusion.55 = f32[32,4096]{1,0:T(8,128)S(1)} fusion(bf16[1024,4096]{1,0:T(8,128)(2,1)} %get-tuple-element.171, bf16[32,1024]{1,0:T(8,128)(2,1)S(1)} %get-tuple-element.157, bf16[32]{0:T(256)(128)(2,1)S(1)} %get-tuple-element.142), kind=kOutput, calls=%fused_computation.24.clone.1 | convolution fusion | flops 268468224 | bytes 8978496 | tf_op jit(solution)/shard_map/while/body/eval_jaxpr/dot_general | solution.py:39
  219.2 1.1 constant_dynamic-slice_fusion.3
  221.4 5.0 %fusion.55 = f32[32,4096]{1,0:T(8,128)S(1)} fusion(bf16[1024,4096]{1,0:T(8,128)(2,1)} %get-tuple-element.171, bf16[32,1024]{1,0:T(8,128)(2,1)S(1)} %get-tuple-element.157, bf16[32]{0:T(256)(128)(2,1)S(1)} %get-tuple-element.142), kind=kOutput, calls=%fused_computation.24.clone.1 | convolution fusion | flops 268468224 | bytes 8978496 | tf_op jit(solution)/shard_map/while/body/eval_jaxpr/dot_general | solution.py:39
  226.4 1.1 constant_dynamic-slice_fusion.3
  228.6 5.0 %fusion.55 = f32[32,4096]{1,0:T(8,128)S(1)} fusion(bf16[1024,4096]{1,0:T(8,128)(2,1)} %get-tuple-element.171, bf16[32,1024]{1,0:T(8,128)(2,1)S(1)} %get-tuple-element.157, bf16[32]{0:T(256)(128)(2,1)S(1)} %get-tuple-element.142), kind=kOutput, calls=%fused_computation.24.clone.1 | convolution fusion | flops 268468224 | bytes 8978496 | tf_op jit(solution)/shard_map/while/body/eval_jaxpr/dot_general | solution.py:39
  233.6 1.1 constant_dynamic-slice_fusion.3
  235.8 5.0 %fusion.55 = f32[32,4096]{1,0:T(8,128)S(1)} fusion(bf16[1024,4096]{1,0:T(8,128)(2,1)} %get-tuple-element.171, bf16[32,1024]{1,0:T(8,128)(2,1)S(1)} %get-tuple-element.157, bf16[32]{0:T(256)(128)(2,1)S(1)} %get-tuple-element.142), kind=kOutput, calls=%fused_computation.24.clone.1 | convolution fusion | flops 268468224 | bytes 8978496 | tf_op jit(solution)/shard_map/while/body/eval_jaxpr/dot_general | solution.py:39
  240.8 1.1 constant_dynamic-slice_fusion.3
  243.0 5.0 %fusion.55 = f32[32,4096]{1,0:T(8,128)S(1)} fusion(bf16[1024,4096]{1,0:T(8,128)(2,1)} %get-tuple-element.171, bf16[32,1024]{1,0:T(8,128)(2,1)S(1)} %get-tuple-element.157, bf16[32]{0:T(256)(128)(2,1)S(1)} %get-tuple-element.142), kind=kOutput, calls=%fused_computation.24.clone.1 | convolution fusion | flops 268468224 | bytes 8978496 | tf_op jit(solution)/shard_map/while/body/eval_jaxpr/dot_general | solution.py:39
  248.0 1.1 constant_dynamic-slice_fusion.3
  250.2 5.0 %fusion.55 = f32[32,4096]{1,0:T(8,128)S(1)} fusion(bf16[1024,4096]{1,0:T(8,128)(2,1)} %get-tuple-element.171, bf16[32,1024]{1,0:T(8,128)(2,1)S(1)} %get-tuple-element.157, bf16[32]{0:T(256)(128)(2,1)S(1)} %get-tuple-element.142), kind=kOutput, calls=%fused_computation.24.clone.1 | convolution fusion | flops 268468224 | bytes 8978496 | tf_op jit(solution)/shard_map/while/body/eval_jaxpr/dot_general | solution.py:39
  255.2 1.1 constant_dynamic-slice_fusion.3
  257.4 5.0 %fusion.55 = f32[32,4096]{1,0:T(8,128)S(1)} fusion(bf16[1024,4096]{1,0:T(8,128)(2,1)} %get-tuple-element.171, bf16[32,1024]{1,0:T(8,128)(2,1)S(1)} %get-tuple-element.157, bf16[32]{0:T(256)(128)(2,1)S(1)} %get-tuple-element.142), kind=kOutput, calls=%fused_computation.24.clone.1 | convolution fusion | flops 268468224 | bytes 8978496 | tf_op jit(solution)/shard_map/while/body/eval_jaxpr/dot_general | solution.py:39
  262.4 1.1 constant_dynamic-slice_fusion.3
  264.6 5.0 %fusion.55 = f32[32,4096]{1,0:T(8,128)S(1)} fusion(bf16[1024,4096]{1,0:T(8,128)(2,1)} %get-tuple-element.171, bf16[32,1024]{1,0:T(8,128)(2,1)S(1)} %get-tuple-element.157, bf16[32]{0:T(256)(128)(2,1)S(1)} %get-tuple-element.142), kind=kOutput, calls=%fused_computation.24.clone.1 | convolution fusion | flops 268468224 | bytes 8978496 | tf_op jit(solution)/shard_map/while/body/eval_jaxpr/dot_general | solution.py:39
  269.6 1.1 constant_dynamic-slice_fusion.3
  271.9 5.0 %fusion.55 = f32[32,4096]{1,0:T(8,128)S(1)} fusion(bf16[1024,4096]{1,0:T(8,128)(2,1)} %get-tuple-element.171, bf16[32,1024]{1,0:T(8,128)(2,1)S(1)} %get-tuple-element.157, bf16[32]{0:T(256)(128)(2,1)S(1)} %get-tuple-element.142), kind=kOutput, calls=%fused_computation.24.clone.1 | convolution fusion | flops 268468224 | bytes 8978496 | tf_op jit(solution)/shard_map/while/body/eval_jaxpr/dot_general | solution.py:39
  276.8 1.1 constant_dynamic-slice_fusion.3
  279.1 5.0 %fusion.55 = f32[32,4096]{1,0:T(8,128)S(1)} fusion(bf16[1024,4096]{1,0:T(8,128)(2,1)} %get-tuple-element.171, bf16[32,1024]{1,0:T(8,128)(2,1)S(1)} %get-tuple-element.157, bf16[32]{0:T(256)(128)(2,1)S(1)} %get-tuple-element.142), kind=kOutput, calls=%fused_computation.24.clone.1 | convolution fusion | flops 268468224 | bytes 8978496 | tf_op jit(solution)/shard_map/while/body/eval_jaxpr/dot_general | solution.py:39
  284.0 1.1 constant_dynamic-slice_fusion.3
  286.3 5.0 %fusion.55 = f32[32,4096]{1,0:T(8,128)S(1)} fusion(bf16[1024,4096]{1,0:T(8,128)(2,1)} %get-tuple-element.171, bf16[32,1024]{1,0:T(8,128)(2,1)S(1)} %get-tuple-element.157, bf16[32]{0:T(256)(128)(2,1)S(1)} %get-tuple-element.142), kind=kOutput, calls=%fused_computation.24.clone.1 | convolution fusion | flops 268468224 | bytes 8978496 | tf_op jit(solution)/shard_map/while/body/eval_jaxpr/dot_general | solution.py:39
  291.2 1.1 constant_dynamic-slice_fusion.3
  293.5 5.0 %fusion.55 = f32[32,4096]{1,0:T(8,128)S(1)} fusion(bf16[1024,4096]{1,0:T(8,128)(2,1)} %get-tuple-element.171, bf16[32,1024]{1,0:T(8,128)(2,1)S(1)} %get-tuple-element.157, bf16[32]{0:T(256)(128)(2,1)S(1)} %get-tuple-element.142), kind=kOutput, calls=%fused_computation.24.clone.1 | convolution fusion | flops 268468224 | bytes 8978496 | tf_op jit(solution)/shard_map/while/body/eval_jaxpr/dot_general | solution.py:39
  298.5 1.1 constant_dynamic-slice_fusion.3
  300.7 5.0 %fusion.55 = f32[32,4096]{1,0:T(8,128)S(1)} fusion(bf16[1024,4096]{1,0:T(8,128)(2,1)} %get-tuple-element.171, bf16[32,1024]{1,0:T(8,128)(2,1)S(1)} %get-tuple-element.157, bf16[32]{0:T(256)(128)(2,1)S(1)} %get-tuple-element.142), kind=kOutput, calls=%fused_computation.24.clone.1 | convolution fusion | flops 268468224 | bytes 8978496 | tf_op jit(solution)/shard_map/while/body/eval_jaxpr/dot_general | solution.py:39
  305.7 1.1 constant_dynamic-slice_fusion.3
  307.9 5.0 %fusion.55 = f32[32,4096]{1,0:T(8,128)S(1)} fusion(bf16[1024,4096]{1,0:T(8,128)(2,1)} %get-tuple-element.171, bf16[32,1024]{1,0:T(8,128)(2,1)S(1)} %get-tuple-element.157, bf16[32]{0:T(256)(128)(2,1)S(1)} %get-tuple-element.142), kind=kOutput, calls=%fused_computation.24.clone.1 | convolution fusion | flops 268468224 | bytes 8978496 | tf_op jit(solution)/shard_map/while/body/eval_jaxpr/dot_general | solution.py:39
  312.9 1.1 constant_dynamic-slice_fusion.3
  315.1 5.0 %fusion.55 = f32[32,4096]{1,0:T(8,128)S(1)} fusion(bf16[1024,4096]{1,0:T(8,128)(2,1)} %get-tuple-element.171, bf16[32,1024]{1,0:T(8,128)(2,1)S(1)} %get-tuple-element.157, bf16[32]{0:T(256)(128)(2,1)S(1)} %get-tuple-element.142), kind=kOutput, calls=%fused_computation.24.clone.1 | convolution fusion | flops 268468224 | bytes 8978496 | tf_op jit(solution)/shard_map/while/body/eval_jaxpr/dot_general | solution.py:39
  320.1 1.1 constant_dynamic-slice_fusion.3
  322.3 5.0 %fusion.55 = f32[32,4096]{1,0:T(8,128)S(1)} fusion(bf16[1024,4096]{1,0:T(8,128)(2,1)} %get-tuple-element.171, bf16[32,1024]{1,0:T(8,128)(2,1)S(1)} %get-tuple-element.157, bf16[32]{0:T(256)(128)(2,1)S(1)} %get-tuple-element.142), kind=kOutput, calls=%fused_computation.24.clone.1 | convolution fusion | flops 268468224 | bytes 8978496 | tf_op jit(solution)/shard_map/while/body/eval_jaxpr/dot_general | solution.py:39
  327.3 1.1 constant_dynamic-slice_fusion.3
  329.5 5.0 %fusion.55 = f32[32,4096]{1,0:T(8,128)S(1)} fusion(bf16[1024,4096]{1,0:T(8,128)(2,1)} %get-tuple-element.171, bf16[32,1024]{1,0:T(8,128)(2,1)S(1)} %get-tuple-element.157, bf16[32]{0:T(256)(128)(2,1)S(1)} %get-tuple-element.142), kind=kOutput, calls=%fused_computation.24.clone.1 | convolution fusion | flops 268468224 | bytes 8978496 | tf_op jit(solution)/shard_map/while/body/eval_jaxpr/dot_general | solution.py:39
  334.5 1.1 constant_dynamic-slice_fusion.3
  336.7 5.0 %fusion.55 = f32[32,4096]{1,0:T(8,128)S(1)} fusion(bf16[1024,4096]{1,0:T(8,128)(2,1)} %get-tuple-element.171, bf16[32,1024]{1,0:T(8,128)(2,1)S(1)} %get-tuple-element.157, bf16[32]{0:T(256)(128)(2,1)S(1)} %get-tuple-element.142), kind=kOutput, calls=%fused_computation.24.clone.1 | convolution fusion | flops 268468224 | bytes 8978496 | tf_op jit(solution)/shard_map/while/body/eval_jaxpr/dot_general | solution.py:39
  341.7 1.1 constant_dynamic-slice_fusion.3
  344.0 5.0 %fusion.55 = f32[32,4096]{1,0:T(8,128)S(1)} fusion(bf16[1024,4096]{1,0:T(8,128)(2,1)} %get-tuple-element.171, bf16[32,1024]{1,0:T(8,128)(2,1)S(1)} %get-tuple-element.157, bf16[32]{0:T(256)(128)(2,1)S(1)} %get-tuple-element.142), kind=kOutput, calls=%fused_computation.24.clone.1 | convolution fusion | flops 268468224 | bytes 8978496 | tf_op jit(solution)/shard_map/while/body/eval_jaxpr/dot_general | solution.py:39
  348.9 1.1 constant_dynamic-slice_fusion.3
  351.2 5.0 %fusion.55 = f32[32,4096]{1,0:T(8,128)S(1)} fusion(bf16[1024,4096]{1,0:T(8,128)(2,1)} %get-tuple-element.171, bf16[32,1024]{1,0:T(8,128)(2,1)S(1)} %get-tuple-element.157, bf16[32]{0:T(256)(128)(2,1)S(1)} %get-tuple-element.142), kind=kOutput, calls=%fused_computation.24.clone.1 | convolution fusion | flops 268468224 | bytes 8978496 | tf_op jit(solution)/shard_map/while/body/eval_jaxpr/dot_general | solution.py:39
  356.1 1.1 constant_dynamic-slice_fusion.3
  358.4 5.0 %fusion.55 = f32[32,4096]{1,0:T(8,128)S(1)} fusion(bf16[1024,4096]{1,0:T(8,128)(2,1)} %get-tuple-element.171, bf16[32,1024]{1,0:T(8,128)(2,1)S(1)} %get-tuple-element.157, bf16[32]{0:T(256)(128)(2,1)S(1)} %get-tuple-element.142), kind=kOutput, calls=%fused_computation.24.clone.1 | convolution fusion | flops 268468224 | bytes 8978496 | tf_op jit(solution)/shard_map/while/body/eval_jaxpr/dot_general | solution.py:39
  363.3 1.1 constant_dynamic-slice_fusion.3
  365.6 5.0 %fusion.55 = f32[32,4096]{1,0:T(8,128)S(1)} fusion(bf16[1024,4096]{1,0:T(8,128)(2,1)} %get-tuple-element.171, bf16[32,1024]{1,0:T(8,128)(2,1)S(1)} %get-tuple-element.157, bf16[32]{0:T(256)(128)(2,1)S(1)} %get-tuple-element.142), kind=kOutput, calls=%fused_computation.24.clone.1 | convolution fusion | flops 268468224 | bytes 8978496 | tf_op jit(solution)/shard_map/while/body/eval_jaxpr/dot_general | solution.py:39
  370.5 1.1 constant_dynamic-slice_fusion.3
  372.8 5.0 %fusion.55 = f32[32,4096]{1,0:T(8,128)S(1)} fusion(bf16[1024,4096]{1,0:T(8,128)(2,1)} %get-tuple-element.171, bf16[32,1024]{1,0:T(8,128)(2,1)S(1)} %get-tuple-element.157, bf16[32]{0:T(256)(128)(2,1)S(1)} %get-tuple-element.142), kind=kOutput, calls=%fused_computation.24.clone.1 | convolution fusion | flops 268468224 | bytes 8978496 | tf_op jit(solution)/shard_map/while/body/eval_jaxpr/dot_general | solution.py:39
  377.8 1.1 constant_dynamic-slice_fusion.3
  380.0 5.0 %fusion.55 = f32[32,4096]{1,0:T(8,128)S(1)} fusion(bf16[1024,4096]{1,0:T(8,128)(2,1)} %get-tuple-element.171, bf16[32,1024]{1,0:T(8,128)(2,1)S(1)} %get-tuple-element.157, bf16[32]{0:T(256)(128)(2,1)S(1)} %get-tuple-element.142), kind=kOutput, calls=%fused_computation.24.clone.1 | convolution fusion | flops 268468224 | bytes 8978496 | tf_op jit(solution)/shard_map/while/body/eval_jaxpr/dot_general | solution.py:39
  385.0 1.1 constant_dynamic-slice_fusion.3
  387.2 2.0 convolution_convert_fusion
  389.2 2.2 reshape.112
  391.5 3.8 copy.48
  395.2 28.5 %all_to_all.30 = bf16[32,2,16,1024]{3,1,2,0:T(2,128)(2,1)S(1)} all-to-all(bf16[32,2,16,1024]{3,1,2,0:T(2,128)(2,1)S(1)} %copy.48), channel_id=1, replica_groups=mesh['batch'=32,'head'=4] {'head'}, dimensions={0} | all-to-all | bytes 4194304 | tf_op jit(solution)/shard_map/all_to_all | solution.py:93
  424.4 8.3 %maximum_convert_fusion = bf16[8,128,1024]{2,1,0:T(8,128)(2,1)S(1)} fusion(bf16[8,128,1024]{2,1,0:T(8,128)(2,1)S(1)} %bitcast.88, bf16[8,1024,1024]{2,1,0:T(8,128)(2,1)} %param.25), kind=kOutput, calls=%fused_computation.31 | convolution fusion | flops 2149580800 | bytes 20971520 | tf_op jit(solution)/shard_map/prh,phk->prk/dot_general | solution.py:96
  434.7 6.6 %all_to_all.31 = bf16[4,2,2304]{2,1,0:T(2,128)(2,1)S(1)} all-to-all(bf16[4,2,2304]{2,1,0:T(2,128)(2,1)S(1)} %reshape.120), channel_id=1, replica_groups=mesh['batch'=32,'head'=4] {'head'}, dimensions={0} | all-to-all | bytes 73728 | tf_op jit(solution)/shard_map/all_to_all | solution.py:107
  (121 shorter events, 34.8 us)
Async XLA Ops:
  7.2 425.5 %copy-start = (bf16[8,512,18]{1,0,2:T(8,128)(2,1)S(1)}, bf16[8,512,18]{1,0,2:T(8,128)(2,1)}, u32[]{:S(2)}) copy-start(bf16[8,512,18]{1,0,2:T(8,128)(2,1)} %param.27) | copy-start | bytes 442372
  7.2 10.6 %copy-start.1 = (bf16[32,24,512]{2,1,0:T(8,128)(2,1)S(1)}, bf16[32,24,512]{2,1,0:T(8,128)(2,1)}, u32[]{:S(2)}) copy-start(bf16[32,24,512]{2,1,0:T(8,128)(2,1)} %param.15) | copy-start | bytes 2359300
  7.2 10.9 %copy-start.9 = (s32[32]{0:T(128)S(1)}, s32[32]{0:T(128)}, u32[]{:S(2)}) copy-start(s32[32]{0:T(128)} %param.18) | copy-start | bytes 388
  7.2 10.9 %copy-start.7 = (s32[32,1]{0,1:T(1,128)S(1)}, s32[32,1]{0,1:T(1,128)}, u32[]{:S(2)}) copy-start(s32[32,1]{0,1:T(1,128)} %param.20) | copy-start | bytes 388
  7.2 11.1 %copy-start.5 = (s32[32,24]{0,1:T(8,128)S(1)}, s32[32,24]{0,1:T(8,128)}, u32[]{:S(2)}) copy-start(s32[32,24]{0,1:T(8,128)} %param.19) | copy-start | bytes 9220
  7.2 11.1 %copy-start.4 = (bf16[32,1024]{1,0:T(8,128)(2,1)S(1)}, bf16[32,1024]{1,0:T(8,128)(2,1)}, u32[]{:S(2)}) copy-start(bf16[32,1024]{1,0:T(8,128)(2,1)} %param.16) | copy-start | bytes 196612
  7.2 11.1 %copy-start.3 = (bf16[32,1024]{1,0:T(8,128)(2,1)S(1)}, bf16[32,1024]{1,0:T(8,128)(2,1)}, u32[]{:S(2)}) copy-start(bf16[32,1024]{1,0:T(8,128)(2,1)} %param.17) | copy-start | bytes 196612
  7.2 90.3 %all-gather.3.cloned.1.call-start = ((), (), s32[]{:S(2)}) async-start(), calls=%async_computation.2 | async-start | bytes 4325376 | tf_op jit(solution)/shard_map/all_gather | solution.py:73
  16.9 185.2 %all-gather.5.cloned.1.call-start = ((), (), s32[]{:S(2)}) async-start(), calls=%async_computation.3 | async-start | bytes 8650752 | tf_op jit(solution)/shard_map/all_gather | solution.py:77
  202.1 12.1 %copy-start.2 = (f32[4,1024]{1,0:T(4,128)S(1)}, f32[4,1024]{1,0:T(4,128)}, u32[]{:S(2)}) copy-start(f32[4,1024]{1,0:T(4,128)} %param.24) | copy-start | bytes 49156
  424.4 8.7 %copy-start.8 = (bf16[8,512]{1,0:T(8,128)(2,1)S(1)}, bf16[8,512]{1,0:T(8,128)(2,1)}, u32[]{:S(2)}) copy-start(bf16[8,512]{1,0:T(8,128)(2,1)} %param.26) | copy-start | bytes 24580
  433.1 9.2 %copy-start.6 = (s32[32,16]{0,1:T(8,128)S(1)}, s32[32,16]{0,1:T(8,128)}, u32[]{:S(2)}) copy-start(s32[32,16]{0,1:T(8,128)} %param.21) | copy-start | bytes 6148
Sparse Core Ops, SparseCore 0:
  17.0 80.4 all-gather.2
  100.6 101.4 all-gather.4
where the time goes:
time: 454 us; the launch traced here: 451 us
  waiting for transfers between devices  144 us (32%)
  matrix products  138 us (30%)
  local copies, waits for them, and re-layouts  82.2 us (18%)
  blocking collectives  43 us (9%)
  other arithmetic  28.7 us (6%)
  between operations  14.3 us (3%)
    dot_general x24, matrix products, lstm_cell(): jnp.dot(full_h, w_flat, preferred_element_type=jnp.float32)  119 us
    all_gather x1, waiting for transfers between devices, shards(): lax.all_gather(w_in_rows, 'batch', axis=0, tiled=True)  79.2 us
    all_gather x1, waiting for transfers between devices, shards(): lax.all_gather(w_rec_rows, 'batch', axis=0, tiled=True)  65.1 us
    all_to_all x1, blocking collectives, shards(): lax.all_to_all(packed, 'head', split_axis=0, concat_axis=1, tiled=True)  28.5 us
    dynamic_slice x24, local copies, waits for them, and re-layouts, shards(): lax.scan(advance, (start_h, start_c.astype(jnp.float32)), (pre, keeps))  26 us
    dynamic_update_slice x24, other arithmetic, shards(): lax.scan(advance, (start_h, start_c.astype(jnp.float32)), (pre, keeps))  19 us
    unnamed x26, local copies, waits for them, and re-layouts  18.5 us
    reshape x1, local copies, waits for them, and re-layouts, shards(): jnp.dot(feat_flat, w_in_full, preferred_element_type=jnp.float32)  15.6 us
  transfers between devices with their start and end apart: 2, of which 2 were waited for; matrix products, arithmetic and copies ran while one was open for 9% of the time, Pallas kernels for 0%

commit v1 on v0

--- a/solution.py
+++ b/solution.py
@@ -90,7 +90,10 @@
         jnp.bfloat16
     )
     packed = packed.reshape(POLICIES, CAPP, learn, width_h)
-    routed = lax.all_to_all(packed, "head", split_axis=0, concat_axis=1, tiled=True)
+    routed = jnp.concatenate(
+        lax.all_to_all(jnp.stack(jnp.split(packed, lax.axis_size("head"), axis=0)), "head", 0, 0),
+        axis=1,
+    )
     local_heads, slots = (routed.shape[0], routed.shape[1])
     rows = routed.reshape(local_heads, slots * learn, width_h)
     mid = jnp.einsum("prh,phk->prk", rows, w_hidden, preferred_element_type=jnp.float32)

time: 454 us -> 438 us (0.965)
  other arithmetic: 28.7 us -> 17.7 us
    dynamic_update_slice x24, other arithmetic: 19 us -> 3.99 us  [shards(): lax.scan(advance, (start_h, start_c.astype(jnp.float32)), (pre, keeps))]
    unnamed x26 -> x28, local copies, waits for them, and re-layouts: 18.5 us -> 18.6 us
where the time goes in v1:
time: 438 us; the launch traced here: 436 us
  waiting for transfers between devices  144 us (33%)
  matrix products  137 us (31%)
  local copies, waits for them, and re-layouts  78.4 us (18%)
  blocking collectives  43 us (10%)
  other arithmetic  17.7 us (4%)
  between operations  14.4 us (3%)
    dot_general x24, matrix products, lstm_cell(): jnp.dot(full_h, w_flat, preferred_element_type=jnp.float32)  119 us
    all_gather x1, waiting for transfers between devices, shards(): lax.all_gather(w_in_rows, 'batch', axis=0, tiled=True)  79.2 us
    all_gather x1, waiting for transfers between devices, shards(): lax.all_gather(w_rec_rows, 'batch', axis=0, tiled=True)  65.1 us
    all_to_all x1, blocking collectives, shards(): lax.all_to_all(jnp.stack(jnp.split(packed, lax.axis_size('head'), axis=0)...  28.5 us
    dynamic_slice x24, local copies, waits for them, and re-layouts, shards(): lax.scan(advance, (start_h, start_c.astype(jnp.float32)), (pre, keeps))  26 us
    unnamed x28, local copies, waits for them, and re-layouts  18.6 us
    reshape x1, local copies, waits for them, and re-layouts, shards(): jnp.dot(feat_flat, w_in_full, preferred_element_type=jnp.float32)  15.6 us
    dot_general x1, local copies, waits for them, and re-layouts, shards(): jnp.dot(feat_flat, w_in_full, preferred_element_type=jnp.float32)  12.7 us
  transfers between devices with their start and end apart: 2, of which 2 were waited for; matrix products, arithmetic and copies ran while one was open for 9% of the time, Pallas kernels for 0%

profile of v1, /device:TPU:1, one launch (start us, length us, event | category | flops | bytes accessed | tf_op | source)
XLA Modules:
  0.0 435.6 jit_solution(2255517060157149244)
XLA Ops:
  7.3 1.0 pad_maximum_fusion.1
  8.3 7.9 %all_gather.9 = bf16[48,4,1024]{2,1,0:T(4,128)(2,1)S(1)} all-gather(bf16[48,4,256]{2,1,0:T(4,128)(2,1)S(1)} %pad_maximum_fusion.1), channel_id=1, replica_groups=mesh['batch'=32,'head'=4] {'head'}, dimensions={2}, use_global_device_ids=true | all-gather | bytes 491520 | tf_op jit(solution)/shard_map/all_gather | solution.py:14
  18.4 79.2 %all-gather.3.cloned.1.call-done = bf16[512,4,1024]{2,1,0:T(4,128)(2,1)} async-done(((bf16[16,4,1024]{2,1,0:T(4,128)(2,1)}), bf16[512,4,1024]{2,1,0:T(4,128)(2,1)}) %all-gather.3.cloned.1.call-update) | async-done | bytes 4194320 | tf_op jit(solution)/shard_map/all_gather | solution.py:73
  97.6 4.5 %copy.59 = bf16[64,8,4,1024]{3,1,2,0:T(8,128)(2,1)S(1)} copy(bf16[64,8,4,1024]{3,2,1,0:T(4,128)(2,1)} %bitcast.95) | data formatting | bytes 8388608
  102.1 6.6 %convolution_bitcast_fusion = f32[768,4096]{0,1:T(8,128)} fusion(bf16[512,4096]{1,0:T(8,128)(2,1)S(1)} %bitcast.96, bf16[768,512]{1,0:T(8,128)(2,1)S(1)} %bitcast.100), kind=kOutput, calls=%fused_computation.30 | convolution fusion | flops 3221225472 | bytes 17563648 | tf_op jit(solution)/shard_map/dot_general | solution.py:74
  108.7 12.7 %copy.46 = f32[768,4096]{1,0:T(8,128)} copy(f32[768,4096]{0,1:T(8,128)} %convolution_bitcast_fusion) | data formatting | bytes 25165824 | tf_op jit(solution)/shard_map/dot_general | solution.py:74
  121.4 15.6 %reshape.115 = f32[24,32,4,1024]{3,2,1,0:T(4,128)} reshape(f32[768,4096]{1,0:T(8,128)} %copy.46) | data formatting | bytes 25165824 | tf_op jit(solution)/shard_map/reshape | solution.py:74
  137.0 65.1 %all-gather.5.cloned.1.call-done = bf16[1024,4,1024]{2,1,0:T(4,128)(2,1)} async-done(((bf16[32,4,1024]{2,1,0:T(4,128)(2,1)}), bf16[1024,4,1024]{2,1,0:T(4,128)(2,1)}) %all-gather.5.cloned.1.call-update) | async-done | bytes 8388624 | tf_op jit(solution)/shard_map/all_gather | solution.py:77
  202.1 12.2 %copy.60 = bf16[128,8,4,1024]{3,1,2,0:T(8,128)(2,1)} copy(bf16[128,8,4,1024]{3,2,1,0:T(4,128)(2,1)} %bitcast.93) | data formatting | bytes 16777216
  214.3 159.0 %while.14 = (s32[]{:T(128)}, bf16[32,1024]{1,0:T(8,128)(2,1)S(1)}, f32[32,1024]{1,0:T(8,128)S(1)}, bf16[24,32,1024]{2,1,0:T(8,128)(2,1)S(1)}, f32[24,32,4,1024]{...) while((s32[]{:T(128)}, bf16[32,1024]{1,0:T(8,128)(2,1)S(1)}, ...), condition=%wide.region_2.3_spmd, body=%wide.region_1.2_spmd.sunk | while | flops 269221920 | bytes 12534761 | solution.py:86
  214.3 5.0 %fusion.56 = f32[32,4096]{1,0:T(8,128)S(1)} fusion(bf16[1024,4096]{1,0:T(8,128)(2,1)} %get-tuple-element.175, bf16[32,1024]{1,0:T(8,128)(2,1)S(1)} %get-tuple-element.161, bf16[32]{0:T(256)(128)(2,1)S(1)} %get-tuple-element.146), kind=kOutput, calls=%fused_computation.24.clone.1 | convolution fusion | flops 268468224 | bytes 8978496 | tf_op jit(solution)/shard_map/while/body/eval_jaxpr/dot_general | solution.py:39
  219.3 1.1 constant_dynamic-slice_fusion.3
  220.9 5.0 %fusion.56 = f32[32,4096]{1,0:T(8,128)S(1)} fusion(bf16[1024,4096]{1,0:T(8,128)(2,1)} %get-tuple-element.175, bf16[32,1024]{1,0:T(8,128)(2,1)S(1)} %get-tuple-element.161, bf16[32]{0:T(256)(128)(2,1)S(1)} %get-tuple-element.146), kind=kOutput, calls=%fused_computation.24.clone.1 | convolution fusion | flops 268468224 | bytes 8978496 | tf_op jit(solution)/shard_map/while/body/eval_jaxpr/dot_general | solution.py:39
  225.9 1.1 constant_dynamic-slice_fusion.3
  227.6 5.0 %fusion.56 = f32[32,4096]{1,0:T(8,128)S(1)} fusion(bf16[1024,4096]{1,0:T(8,128)(2,1)} %get-tuple-element.175, bf16[32,1024]{1,0:T(8,128)(2,1)S(1)} %get-tuple-element.161, bf16[32]{0:T(256)(128)(2,1)S(1)} %get-tuple-element.146), kind=kOutput, calls=%fused_computation.24.clone.1 | convolution fusion | flops 268468224 | bytes 8978496 | tf_op jit(solution)/shard_map/while/body/eval_jaxpr/dot_general | solution.py:39
  232.5 1.1 constant_dynamic-slice_fusion.3
  234.2 5.0 %fusion.56 = f32[32,4096]{1,0:T(8,128)S(1)} fusion(bf16[1024,4096]{1,0:T(8,128)(2,1)} %get-tuple-element.175, bf16[32,1024]{1,0:T(8,128)(2,1)S(1)} %get-tuple-element.161, bf16[32]{0:T(256)(128)(2,1)S(1)} %get-tuple-element.146), kind=kOutput, calls=%fused_computation.24.clone.1 | convolution fusion | flops 268468224 | bytes 8978496 | tf_op jit(solution)/shard_map/while/body/eval_jaxpr/dot_general | solution.py:39
  239.1 1.1 constant_dynamic-slice_fusion.3
  240.8 5.0 %fusion.56 = f32[32,4096]{1,0:T(8,128)S(1)} fusion(bf16[1024,4096]{1,0:T(8,128)(2,1)} %get-tuple-element.175, bf16[32,1024]{1,0:T(8,128)(2,1)S(1)} %get-tuple-element.161, bf16[32]{0:T(256)(128)(2,1)S(1)} %get-tuple-element.146), kind=kOutput, calls=%fused_computation.24.clone.1 | convolution fusion | flops 268468224 | bytes 8978496 | tf_op jit(solution)/shard_map/while/body/eval_jaxpr/dot_general | solution.py:39
  245.8 1.1 constant_dynamic-slice_fusion.3
  247.4 5.0 %fusion.56 = f32[32,4096]{1,0:T(8,128)S(1)} fusion(bf16[1024,4096]{1,0:T(8,128)(2,1)} %get-tuple-element.175, bf16[32,1024]{1,0:T(8,128)(2,1)S(1)} %get-tuple-element.161, bf16[32]{0:T(256)(128)(2,1)S(1)} %get-tuple-element.146), kind=kOutput, calls=%fused_computation.24.clone.1 | convolution fusion | flops 268468224 | bytes 8978496 | tf_op jit(solution)/shard_map/while/body/eval_jaxpr/dot_general | solution.py:39
  252.4 1.1 constant_dynamic-slice_fusion.3
  254.0 5.0 %fusion.56 = f32[32,4096]{1,0:T(8,128)S(1)} fusion(bf16[1024,4096]{1,0:T(8,128)(2,1)} %get-tuple-element.175, bf16[32,1024]{1,0:T(8,128)(2,1)S(1)} %get-tuple-element.161, bf16[32]{0:T(256)(128)(2,1)S(1)} %get-tuple-element.146), kind=kOutput, calls=%fused_computation.24.clone.1 | convolution fusion | flops 268468224 | bytes 8978496 | tf_op jit(solution)/shard_map/while/body/eval_jaxpr/dot_general | solution.py:39
  259.0 1.1 constant_dynamic-slice_fusion.3
  260.6 5.0 %fusion.56 = f32[32,4096]{1,0:T(8,128)S(1)} fusion(bf16[1024,4096]{1,0:T(8,128)(2,1)} %get-tuple-element.175, bf16[32,1024]{1,0:T(8,128)(2,1)S(1)} %get-tuple-element.161, bf16[32]{0:T(256)(128)(2,1)S(1)} %get-tuple-element.146), kind=kOutput, calls=%fused_computation.24.clone.1 | convolution fusion | flops 268468224 | bytes 8978496 | tf_op jit(solution)/shard_map/while/body/eval_jaxpr/dot_general | solution.py:39
  265.6 1.1 constant_dynamic-slice_fusion.3
  267.3 5.0 %fusion.56 = f32[32,4096]{1,0:T(8,128)S(1)} fusion(bf16[1024,4096]{1,0:T(8,128)(2,1)} %get-tuple-element.175, bf16[32,1024]{1,0:T(8,128)(2,1)S(1)} %get-tuple-element.161, bf16[32]{0:T(256)(128)(2,1)S(1)} %get-tuple-element.146), kind=kOutput, calls=%fused_computation.24.clone.1 | convolution fusion | flops 268468224 | bytes 8978496 | tf_op jit(solution)/shard_map/while/body/eval_jaxpr/dot_general | solution.py:39
  272.2 1.1 constant_dynamic-slice_fusion.3
  273.9 5.0 %fusion.56 = f32[32,4096]{1,0:T(8,128)S(1)} fusion(bf16[1024,4096]{1,0:T(8,128)(2,1)} %get-tuple-element.175, bf16[32,1024]{1,0:T(8,128)(2,1)S(1)} %get-tuple-element.161, bf16[32]{0:T(256)(128)(2,1)S(1)} %get-tuple-element.146), kind=kOutput, calls=%fused_computation.24.clone.1 | convolution fusion | flops 268468224 | bytes 8978496 | tf_op jit(solution)/shard_map/while/body/eval_jaxpr/dot_general | solution.py:39
  278.8 1.1 constant_dynamic-slice_fusion.3
  280.5 5.0 %fusion.56 = f32[32,4096]{1,0:T(8,128)S(1)} fusion(bf16[1024,4096]{1,0:T(8,128)(2,1)} %get-tuple-element.175, bf16[32,1024]{1,0:T(8,128)(2,1)S(1)} %get-tuple-element.161, bf16[32]{0:T(256)(128)(2,1)S(1)} %get-tuple-element.146), kind=kOutput, calls=%fused_computation.24.clone.1 | convolution fusion | flops 268468224 | bytes 8978496 | tf_op jit(solution)/shard_map/while/body/eval_jaxpr/dot_general | solution.py:39
  285.5 1.1 constant_dynamic-slice_fusion.3
  287.1 5.0 %fusion.56 = f32[32,4096]{1,0:T(8,128)S(1)} fusion(bf16[1024,4096]{1,0:T(8,128)(2,1)} %get-tuple-element.175, bf16[32,1024]{1,0:T(8,128)(2,1)S(1)} %get-tuple-element.161, bf16[32]{0:T(256)(128)(2,1)S(1)} %get-tuple-element.146), kind=kOutput, calls=%fused_computation.24.clone.1 | convolution fusion | flops 268468224 | bytes 8978496 | tf_op jit(solution)/shard_map/while/body/eval_jaxpr/dot_general | solution.py:39
  292.1 1.1 constant_dynamic-slice_fusion.3
  293.7 5.0 %fusion.56 = f32[32,4096]{1,0:T(8,128)S(1)} fusion(bf16[1024,4096]{1,0:T(8,128)(2,1)} %get-tuple-element.175, bf16[32,1024]{1,0:T(8,128)(2,1)S(1)} %get-tuple-element.161, bf16[32]{0:T(256)(128)(2,1)S(1)} %get-tuple-element.146), kind=kOutput, calls=%fused_computation.24.clone.1 | convolution fusion | flops 268468224 | bytes 8978496 | tf_op jit(solution)/shard_map/while/body/eval_jaxpr/dot_general | solution.py:39
  298.7 1.1 constant_dynamic-slice_fusion.3
  300.3 5.0 %fusion.56 = f32[32,4096]{1,0:T(8,128)S(1)} fusion(bf16[1024,4096]{1,0:T(8,128)(2,1)} %get-tuple-element.175, bf16[32,1024]{1,0:T(8,128)(2,1)S(1)} %get-tuple-element.161, bf16[32]{0:T(256)(128)(2,1)S(1)} %get-tuple-element.146), kind=kOutput, calls=%fused_computation.24.clone.1 | convolution fusion | flops 268468224 | bytes 8978496 | tf_op jit(solution)/shard_map/while/body/eval_jaxpr/dot_general | solution.py:39
  305.3 1.1 constant_dynamic-slice_fusion.3
  307.0 5.0 %fusion.56 = f32[32,4096]{1,0:T(8,128)S(1)} fusion(bf16[1024,4096]{1,0:T(8,128)(2,1)} %get-tuple-element.175, bf16[32,1024]{1,0:T(8,128)(2,1)S(1)} %get-tuple-element.161, bf16[32]{0:T(256)(128)(2,1)S(1)} %get-tuple-element.146), kind=kOutput, calls=%fused_computation.24.clone.1 | convolution fusion | flops 268468224 | bytes 8978496 | tf_op jit(solution)/shard_map/while/body/eval_jaxpr/dot_general | solution.py:39
  311.9 1.1 constant_dynamic-slice_fusion.3
  313.6 5.0 %fusion.56 = f32[32,4096]{1,0:T(8,128)S(1)} fusion(bf16[1024,4096]{1,0:T(8,128)(2,1)} %get-tuple-element.175, bf16[32,1024]{1,0:T(8,128)(2,1)S(1)} %get-tuple-element.161, bf16[32]{0:T(256)(128)(2,1)S(1)} %get-tuple-element.146), kind=kOutput, calls=%fused_computation.24.clone.1 | convolution fusion | flops 268468224 | bytes 8978496 | tf_op jit(solution)/shard_map/while/body/eval_jaxpr/dot_general | solution.py:39
  318.5 1.1 constant_dynamic-slice_fusion.3
  320.2 5.0 %fusion.56 = f32[32,4096]{1,0:T(8,128)S(1)} fusion(bf16[1024,4096]{1,0:T(8,128)(2,1)} %get-tuple-element.175, bf16[32,1024]{1,0:T(8,128)(2,1)S(1)} %get-tuple-element.161, bf16[32]{0:T(256)(128)(2,1)S(1)} %get-tuple-element.146), kind=kOutput, calls=%fused_computation.24.clone.1 | convolution fusion | flops 268468224 | bytes 8978496 | tf_op jit(solution)/shard_map/while/body/eval_jaxpr/dot_general | solution.py:39
  325.2 1.1 constant_dynamic-slice_fusion.3
  326.8 5.0 %fusion.56 = f32[32,4096]{1,0:T(8,128)S(1)} fusion(bf16[1024,4096]{1,0:T(8,128)(2,1)} %get-tuple-element.175, bf16[32,1024]{1,0:T(8,128)(2,1)S(1)} %get-tuple-element.161, bf16[32]{0:T(256)(128)(2,1)S(1)} %get-tuple-element.146), kind=kOutput, calls=%fused_computation.24.clone.1 | convolution fusion | flops 268468224 | bytes 8978496 | tf_op jit(solution)/shard_map/while/body/eval_jaxpr/dot_general | solution.py:39
  331.8 1.1 constant_dynamic-slice_fusion.3
  333.4 5.0 %fusion.56 = f32[32,4096]{1,0:T(8,128)S(1)} fusion(bf16[1024,4096]{1,0:T(8,128)(2,1)} %get-tuple-element.175, bf16[32,1024]{1,0:T(8,128)(2,1)S(1)} %get-tuple-element.161, bf16[32]{0:T(256)(128)(2,1)S(1)} %get-tuple-element.146), kind=kOutput, calls=%fused_computation.24.clone.1 | convolution fusion | flops 268468224 | bytes 8978496 | tf_op jit(solution)/shard_map/while/body/eval_jaxpr/dot_general | solution.py:39
  338.4 1.1 constant_dynamic-slice_fusion.3
  340.0 5.0 %fusion.56 = f32[32,4096]{1,0:T(8,128)S(1)} fusion(bf16[1024,4096]{1,0:T(8,128)(2,1)} %get-tuple-element.175, bf16[32,1024]{1,0:T(8,128)(2,1)S(1)} %get-tuple-element.161, bf16[32]{0:T(256)(128)(2,1)S(1)} %get-tuple-element.146), kind=kOutput, calls=%fused_computation.24.clone.1 | convolution fusion | flops 268468224 | bytes 8978496 | tf_op jit(solution)/shard_map/while/body/eval_jaxpr/dot_general | solution.py:39
  345.0 1.1 constant_dynamic-slice_fusion.3
  346.7 5.0 %fusion.56 = f32[32,4096]{1,0:T(8,128)S(1)} fusion(bf16[1024,4096]{1,0:T(8,128)(2,1)} %get-tuple-element.175, bf16[32,1024]{1,0:T(8,128)(2,1)S(1)} %get-tuple-element.161, bf16[32]{0:T(256)(128)(2,1)S(1)} %get-tuple-element.146), kind=kOutput, calls=%fused_computation.24.clone.1 | convolution fusion | flops 268468224 | bytes 8978496 | tf_op jit(solution)/shard_map/while/body/eval_jaxpr/dot_general | solution.py:39
  351.6 1.1 constant_dynamic-slice_fusion.3
  353.3 5.0 %fusion.56 = f32[32,4096]{1,0:T(8,128)S(1)} fusion(bf16[1024,4096]{1,0:T(8,128)(2,1)} %get-tuple-element.175, bf16[32,1024]{1,0:T(8,128)(2,1)S(1)} %get-tuple-element.161, bf16[32]{0:T(256)(128)(2,1)S(1)} %get-tuple-element.146), kind=kOutput, calls=%fused_computation.24.clone.1 | convolution fusion | flops 268468224 | bytes 8978496 | tf_op jit(solution)/shard_map/while/body/eval_jaxpr/dot_general | solution.py:39
  358.2 1.1 constant_dynamic-slice_fusion.3
  359.9 5.0 %fusion.56 = f32[32,4096]{1,0:T(8,128)S(1)} fusion(bf16[1024,4096]{1,0:T(8,128)(2,1)} %get-tuple-element.175, bf16[32,1024]{1,0:T(8,128)(2,1)S(1)} %get-tuple-element.161, bf16[32]{0:T(256)(128)(2,1)S(1)} %get-tuple-element.146), kind=kOutput, calls=%fused_computation.24.clone.1 | convolution fusion | flops 268468224 | bytes 8978496 | tf_op jit(solution)/shard_map/while/body/eval_jaxpr/dot_general | solution.py:39
  364.9 1.1 constant_dynamic-slice_fusion.3
  366.5 5.0 %fusion.56 = f32[32,4096]{1,0:T(8,128)S(1)} fusion(bf16[1024,4096]{1,0:T(8,128)(2,1)} %get-tuple-element.175, bf16[32,1024]{1,0:T(8,128)(2,1)S(1)} %get-tuple-element.161, bf16[32]{0:T(256)(128)(2,1)S(1)} %get-tuple-element.146), kind=kOutput, calls=%fused_computation.24.clone.1 | convolution fusion | flops 268468224 | bytes 8978496 | tf_op jit(solution)/shard_map/while/body/eval_jaxpr/dot_general | solution.py:39
  371.5 1.1 constant_dynamic-slice_fusion.3
  375.2 3.9 pad_maximum_fusion
  379.0 28.5 %all_to_all.20 = bf16[4,8,2,16,1024]{4,2,1,3,0:T(2,128)(2,1)S(1)} all-to-all(bf16[4,8,2,16,1024]{4,2,1,3,0:T(2,128)(2,1)S(1)} %pad_maximum_fusion), channel_id=1, replica_groups=mesh['batch'=32,'head'=4] {'head'}, dimensions={0} | all-to-all | bytes 4194304 | tf_op jit(solution)/shard_map/all_to_all | solution.py:94
  407.5 1.7 copy.47
  409.3 8.3 %maximum_convert_fusion = bf16[8,128,1024]{2,1,0:T(8,128)(2,1)S(1)} fusion(bf16[8,128,1024]{2,1,0:T(8,128)(2,1)S(1)} %bitcast.92, bf16[8,1024,1024]{2,1,0:T(8,128)(2,1)} %param.25), kind=kOutput, calls=%fused_computation.31 | convolution fusion | flops 2149580800 | bytes 20971520 | tf_op jit(solution)/shard_map/prh,phk->prk/dot_general | solution.py:99
  419.6 6.6 %all_to_all.21 = bf16[4,2,2304]{2,1,0:T(2,128)(2,1)S(1)} all-to-all(bf16[4,2,2304]{2,1,0:T(2,128)(2,1)S(1)} %reshape.124), channel_id=1, replica_groups=mesh['batch'=32,'head'=4] {'head'}, dimensions={0} | all-to-all | bytes 73728 | tf_op jit(solution)/shard_map/all_to_all | solution.py:110
  427.2 0.9 select_reduce_fusion
  (127 shorter events, 20.2 us)
Async XLA Ops:
  7.2 410.4 %copy-start = (bf16[8,512,18]{1,0,2:T(8,128)(2,1)S(1)}, bf16[8,512,18]{1,0,2:T(8,128)(2,1)}, u32[]{:S(2)}) copy-start(bf16[8,512,18]{1,0,2:T(8,128)(2,1)} %param.27) | copy-start | bytes 442372
  7.2 10.6 %copy-start.1 = (bf16[32,24,512]{2,1,0:T(8,128)(2,1)S(1)}, bf16[32,24,512]{2,1,0:T(8,128)(2,1)}, u32[]{:S(2)}) copy-start(bf16[32,24,512]{2,1,0:T(8,128)(2,1)} %param.15) | copy-start | bytes 2359300
  7.2 10.9 %copy-start.10 = (s32[32]{0:T(128)S(1)}, s32[32]{0:T(128)}, u32[]{:S(2)}) copy-start(s32[32]{0:T(128)} %param.18) | copy-start | bytes 388
  7.2 10.9 %copy-start.8 = (s32[32,1]{0,1:T(1,128)S(1)}, s32[32,1]{0,1:T(1,128)}, u32[]{:S(2)}) copy-start(s32[32,1]{0,1:T(1,128)} %param.20) | copy-start | bytes 388
  7.2 11.1 %copy-start.6 = (s32[32,24]{0,1:T(8,128)S(1)}, s32[32,24]{0,1:T(8,128)}, u32[]{:S(2)}) copy-start(s32[32,24]{0,1:T(8,128)} %param.19) | copy-start | bytes 9220
  7.2 11.1 %copy-start.5 = (bf16[32,1024]{1,0:T(8,128)(2,1)S(1)}, bf16[32,1024]{1,0:T(8,128)(2,1)}, u32[]{:S(2)}) copy-start(bf16[32,1024]{1,0:T(8,128)(2,1)} %param.16) | copy-start | bytes 196612
  7.2 11.1 %copy-start.4 = (bf16[32,1024]{1,0:T(8,128)(2,1)S(1)}, bf16[32,1024]{1,0:T(8,128)(2,1)}, u32[]{:S(2)}) copy-start(bf16[32,1024]{1,0:T(8,128)(2,1)} %param.17) | copy-start | bytes 196612
  7.2 90.3 %all-gather.3.cloned.1.call-start = ((), (), s32[]{:S(2)}) async-start(), calls=%async_computation.2 | async-start | bytes 4325376 | tf_op jit(solution)/shard_map/all_gather | solution.py:73
  16.9 185.2 %all-gather.5.cloned.1.call-start = ((), (), s32[]{:S(2)}) async-start(), calls=%async_computation.3 | async-start | bytes 8650752 | tf_op jit(solution)/shard_map/all_gather | solution.py:77
  202.1 12.2 %copy-start.2 = (bf16[24,32,1024]{2,1,0:T(8,128)(2,1)S(1)}, bf16[24,32,1024]{2,1,0:T(8,128)(2,1)}, u32[]{:S(2)}) copy-start(bf16[24,32,1024]{2,1,0:T(8,128)(2,1)} %custom-call) | copy-start | bytes 4718596
  202.1 12.2 %copy-start.3 = (f32[4,1024]{1,0:T(4,128)S(1)}, f32[4,1024]{1,0:T(4,128)}, u32[]{:S(2)}) copy-start(f32[4,1024]{1,0:T(4,128)} %param.24) | copy-start | bytes 49156
  409.3 8.7 %copy-start.9 = (bf16[8,512]{1,0:T(8,128)(2,1)S(1)}, bf16[8,512]{1,0:T(8,128)(2,1)}, u32[]{:S(2)}) copy-start(bf16[8,512]{1,0:T(8,128)(2,1)} %param.26) | copy-start | bytes 24580
  418.0 9.2 %copy-start.7 = (s32[32,16]{0,1:T(8,128)S(1)}, s32[32,16]{0,1:T(8,128)}, u32[]{:S(2)}) copy-start(s32[32,16]{0,1:T(8,128)} %param.21) | copy-start | bytes 6148
Sparse Core Ops, SparseCore 0:
  17.0 80.4 all-gather.2
  100.6 101.4 all-gather.4
